TPU v7x, 256 devices: a whole 4x4x8 slice. The times are simulated.
256 devices in a mesh: cut: 32 (over z, y), sub: 8 (over x, core).
Axes of the slice: x: 4, y: 4, z: 8, core: 2. Of those that a mesh axis runs over, the one named last changes fastest.
Arguments:
- residual: bfloat16 [32, 8, 1024, 128], P('cut', 'sub'), may hold values from -6 to 6
- inner_inverse: bfloat16 [32, 8, 4, 343, 343], P('cut', 'sub'), may hold values from -0.3125 to 0.3125
- inner_index: int32 [32, 8, 4, 343], P('cut', 'sub'), may hold values from 0 to 1023
- slab_dofs: int32 [32, 8, 5, 512], P('cut', 'sub'), may hold values from 0 to 1023
- face_inverse: bfloat16 [32, 8, 5, 3, 343, 343], P('cut', 'sub'), may hold values from -0.3125 to 0.3125
- face_index: int32 [32, 8, 5, 3, 343], P('cut', 'sub'), may hold values from 0 to 1023
- face_count: int32 [32, 8, 5], P('cut', 'sub'), may hold values from 1 to 3
Outputs:
- correction: float32 [32, 8, 1024, 128], P('cut', 'sub')
All inputs are finite; a program needn't handle non-finite values.
Results may differ from a plain program's by a relative error of at most 0.0003.
Values may be sent and summed in bfloat16 or wider, within the bound.
A program may use at most 64 MiB of HBM per device.

v0:
```python
import functools

import jax
import jax.numpy as jnp
from jax import lax
from jax.experimental import pallas as pl
from jax.experimental.pallas import tpu as pltpu
from jax.sharding import PartitionSpec as P

MESH = pl.DeviceIdType.MESH
CUTLV = 3
LANES = 128
SEND_ORDER = (0, 1, 2, 3, 4)
WORK_ORDER = (4, 0, 1, 2, 3)
BF = jnp.bfloat16
F32 = jnp.float32


def dot(a, b):
    return jnp.dot(a, b, preferred_element_type=F32)


def hi_lo(x):
    hi = x.astype(BF)
    lo = (x - hi.astype(F32)).astype(BF)
    return jnp.concatenate([hi, lo], axis=1)


def columns(row):
    n = row.shape[1]
    return jnp.transpose(jnp.broadcast_to(row, (LANES, n)))


def pick(col, wide):
    half = wide.shape[0]
    low = col & (half - 1)
    lane = lax.broadcasted_iota(jnp.int32, col.shape, 1)
    hot = jnp.concatenate(
        [jnp.where(low == lane + LANES * t, 1.0, 0.0).astype(BF) for t in range(half // LANES)],
        axis=1,
    )
    got = dot(hot, wide)
    return jnp.where(col >= half, got[:, LANES:], got[:, :LANES]).astype(BF)


def kernel(
    cut_bits, sub_bits, levels, stars, inner,
    res_h, imat_h, iidx_h, dofs_h, fmat_h, fidx_h, cnt_h, out_ref,
    res, imat, iidx, dofs, fmat, fidx, cnt,
    own, far, kept, sent, sent_scale, got, got_scale, acc,
    ipad, fpad, ihot, fhot, dhot, ystar,
    lsem, ssem, rsem,
):
    c = lax.axis_index("cut")
    b = lax.axis_index("sub")
    star = fidx.shape[2]
    pad = fpad.shape[2]
    slab = own.shape[1]
    ndof = res.shape[0]

    def far_device(level):
        if level < CUTLV:
            return (c ^ (1 << (cut_bits - 1 - level)), b)
        return (c, b ^ (1 << (sub_bits - 1 - (level - CUTLV))))

    def upper(level):
        if level < CUTLV:
            return (c >> (cut_bits - 1 - level)) & 1
        return (b >> (sub_bits - 1 - (level - CUTLV))) & 1

    barrier = pltpu.get_barrier_semaphore()
    for level in range(levels):
        pl.semaphore_signal(barrier, inc=1, device_id=far_device(level), device_id_type=MESH)
    small = [
        pltpu.make_async_copy(a, d, lsem.at[i])
        for i, (a, d) in enumerate(
            ((dofs_h, dofs), (res_h, res), (fidx_h, fidx), (iidx_h, iidx), (cnt_h, cnt), (imat_h, imat))
        )
    ]
    big = [
        pltpu.make_async_copy(
            fmat_h.at[pl.ds(k * stars, stars)], fmat.at[pl.ds(k * stars, stars)], lsem.at[6 + k]
        )
        for k in range(levels)
    ]
    for copy in small + big:
        copy.start()
    ystar[...] = jnp.zeros_like(ystar)
    ipad[...] = jnp.full_like(ipad, -1)
    fpad[...] = jnp.full_like(fpad, -1)
    small[0].wait()
    small[1].wait()
    wide_res = jnp.concatenate([res[: ndof // 2], res[ndof // 2 :]], axis=1)

    def slab_step(k, _):
        own[k] = pick(columns(dofs[k]), wide_res)
        return 0

    lax.fori_loop(0, levels, slab_step, 0)

    pl.semaphore_wait(barrier, levels)
    slab_copy = {}
    for level in SEND_ORDER:
        slab_copy[level] = pltpu.make_async_remote_copy(
            src_ref=own.at[level], dst_ref=far.at[level],
            send_sem=ssem.at[level], recv_sem=rsem.at[level],
            device_id=far_device(level), device_id_type=MESH,
        )
        slab_copy[level].start()

    for i in range(2, 5):
        small[i].wait()
    for n in range(inner):
        ipad[n, :, 0:star] = iidx[n : n + 1, :]
    for level in range(levels):
        flip = slab * (1 - upper(level))
        for j in range(stars):
            fpad[level * stars + j, :, 0:star] = fidx[level * stars + j] ^ flip

    block = LANES

    def inner_hot(i, _):
        at = pl.multiple_of(i * block, block)
        for n in range(inner):
            row = jnp.broadcast_to(ipad[n], (block, pad))
            place = lax.broadcasted_iota(jnp.int32, (block, pad), 0) + at
            ihot[pl.ds(at, block), n * pad : (n + 1) * pad] = jnp.where(row == place, 1.0, 0.0).astype(BF)
        return 0

    lax.fori_loop(0, ndof // block, inner_hot, 0)

    small[5].wait()
    for n in range(inner):
        g = pick(columns(ipad[n]), wide_res)
        y = dot(imat[:, n, :], g[:star])
        ystar[n * pad : n * pad + star, :] = hi_lo(y)

    def inner_scatter(i, _):
        at = pl.multiple_of(i * block, block)
        z = dot(ihot[pl.ds(at, block), :], ystar[...])
        acc[pl.ds(at, block), :] = z[:, :LANES] + z[:, LANES:]
        return 0

    lax.fori_loop(0, ndof // block, inner_scatter, 0)

    for level in range(levels):
        live = cnt[0:1, level : level + 1]

        def face_hot(i, _, level=level, live=live):
            at = pl.multiple_of(i * block, block)
            for j in range(stars):
                index = jnp.where(jnp.broadcast_to(live, (1, pad)) > j, fpad[level * stars + j], -1)
                row = jnp.broadcast_to(index, (block, pad))
                place = lax.broadcasted_iota(jnp.int32, (block, pad), 0) + at
                fhot[level, pl.ds(at, block), j * pad : (j + 1) * pad] = jnp.where(
                    row == place, 1.0, 0.0
                ).astype(BF)
            row = jnp.broadcast_to(dofs[level], (block, slab))
            place = lax.broadcasted_iota(jnp.int32, (block, slab), 0) + at
            dhot[level, pl.ds(at, block), :] = jnp.where(row == place, 1.0, 0.0).astype(BF)
            return 0

        lax.fori_loop(0, ndof // block, face_hot, 0)

    data_copy, scale_copy = {}, {}
    used = stars * pad
    for level in WORK_ORDER:
        big[level].wait()
        slab_copy[level].wait_recv()
        wide = jnp.concatenate([far[level], own[level]], axis=1)
        for j in range(stars):
            g = pick(columns(fpad[level * stars + j]), wide)
            y = dot(fmat[level * stars + j], g[:star])
            ystar[j * pad : j * pad + star, :] = hi_lo(y)
        z = dot(fhot[level, 0:slab, :], ystar[0:used, :])
        give = z[:, :LANES] + z[:, LANES:]
        tiles = give.reshape(slab // 8, 8, LANES)
        top = jnp.max(jnp.abs(tiles), axis=0)
        scale = jnp.where(top > 0.0, 1.0 / top, 0.0)
        coded = jnp.round((tiles * scale[None]) * 32767.0).astype(jnp.int32)
        sent[level] = coded.reshape(slab, LANES).astype(jnp.int16)
        sent_scale[level] = top
        for copies, src, dst, at in (
            (data_copy, sent, got, levels),
            (scale_copy, sent_scale, got_scale, 2 * levels),
        ):
            copies[level] = pltpu.make_async_remote_copy(
                src_ref=src.at[level], dst_ref=dst.at[level],
                send_sem=ssem.at[at + level], recv_sem=rsem.at[at + level],
                device_id=far_device(level), device_id_type=MESH,
            )
            copies[level].start()
        z = dot(fhot[level, slab:, :], ystar[0:used, :])
        kept[level] = z[:, :LANES] + z[:, LANES:]

    for level in WORK_ORDER:
        data_copy[level].wait_recv()
        scale_copy[level].wait_recv()
        tiles = got[level].astype(jnp.int32).astype(F32).reshape(slab // 8, 8, LANES)
        back = (tiles * (1.0 / 32767.0)) * got_scale[level][None]
        ystar[0:slab, :] = hi_lo(kept[level] + back.reshape(slab, LANES))

        def spread(i, _, level=level):
            at = pl.multiple_of(i * block, block)
            z = dot(dhot[level, pl.ds(at, block), :], ystar[0:slab, :])
            acc[pl.ds(at, block), :] += z[:, :LANES] + z[:, LANES:]
            return 0

        lax.fori_loop(0, ndof // block, spread, 0)
    out_ref[...] = acc[...]
    for level in range(levels):
        slab_copy[level].wait_send()
        data_copy[level].wait_send()
        scale_copy[level].wait_send()


def on_device(residual, inner_inverse, inner_index, slab_dofs, face_inverse, face_index, face_count):
    ndof, width = residual.shape[2:]
    inner, star = inner_index.shape[2:]
    levels, slab = slab_dofs.shape[2:]
    stars = face_index.shape[3]
    pad = -(-star // LANES) * LANES
    cut_bits = lax.axis_size("cut").bit_length() - 1
    sub_bits = lax.axis_size("sub").bit_length() - 1
    i32 = jnp.int32
    vm = pltpu.VMEM
    out = pl.pallas_call(
        functools.partial(kernel, cut_bits, sub_bits, levels, stars, inner),
        out_shape=jax.ShapeDtypeStruct((ndof, width), F32),
        in_specs=[pl.BlockSpec(memory_space=pl.ANY)] * 7,
        out_specs=pl.BlockSpec(memory_space=pltpu.VMEM),
        scratch_shapes=[
            vm((ndof, width), BF),
            vm((star, inner, star), BF),
            vm((inner, star), i32),
            vm((levels, 1, slab), i32),
            vm((levels * stars, star, star), BF),
            vm((levels * stars, 1, star), i32),
            vm((1, levels), i32),
            vm((levels, slab, width), BF),
            vm((levels, slab, width), BF),
            vm((levels, slab, width), F32),
            vm((levels, slab, width), jnp.int16),
            vm((levels, 8, width), F32),
            vm((levels, slab, width), jnp.int16),
            vm((levels, 8, width), F32),
            vm((ndof, width), F32),
            vm((inner, 1, pad), i32),
            vm((levels * stars, 1, pad), i32),
            vm((ndof, inner * pad), BF),
            vm((levels, ndof, stars * pad), BF),
            vm((levels, ndof, slab), BF),
            vm((inner * pad, 2 * width), BF),
            pltpu.SemaphoreType.DMA((6 + levels,)),
            pltpu.SemaphoreType.DMA((3 * levels,)),
            pltpu.SemaphoreType.DMA((3 * levels,)),
        ],
        compiler_params=pltpu.CompilerParams(
            collective_id=0, has_side_effects=True, vmem_limit_bytes=60 * 1024 * 1024
        ),
    )(
        residual[0, 0],
        jnp.transpose(inner_inverse[0, 0], (1, 0, 2)),
        inner_index[0, 0],
        slab_dofs[0, 0][:, None, :],
        face_inverse[0, 0].reshape(levels * stars, star, star),
        face_index[0, 0].reshape(levels * stars, 1, star),
        face_count[0],
    )
    return out[None, None]


def solution(mesh):
    return jax.shard_map(
        on_device,
        mesh=mesh,
        in_specs=(
            P("cut", "sub", None, None),
            P("cut", "sub", None, None, None),
            P("cut", "sub", None, None),
            P("cut", "sub", None, None),
            P("cut", "sub", None, None, None, None),
            P("cut", "sub", None, None, None),
            P("cut", "sub", None),
        ),
        out_specs=P("cut", "sub", None, None),
        check_vma=False,
    )
```

profile of v0, /device:TPU:1, one launch (start us, length us, event | category | flops | bytes accessed | tf_op | source)
XLA Modules:
  0.0 47.4 jit_solution(9031824651050318603)
XLA Ops:
  0.0 45.6 %shard_map.73 = f32[1024,128]{1,0:T(8,128)} custom-call(bf16[1024,128]{1,0:T(8,128)(2,1)} %bitcast.13, bf16[343,4,343]{2,1,0:T(4,128)(2,1)} %bitcast.12, s32[4,343]{1,0:T(4,128)} %bitcast.16, s32[5,1,512]{2,1,0:T(1,128)} %bitcast.15, bf16[15,343,343]{2,1,0:T(8,128)(2,1)} %bitcast.10, s32[15,1,343]{2,1,0:T(1,128)} %bitcast.14, s32[1,5]{1,0:T(1,128)} %bitcast.17), custom_call_target="tpu_custom_call" | custom-call | tf_op jit(solution)/shard_map/pallas_call | solution.py:227
  45.6 1.9 %copy.9 = f32[1,1,1024,128]{3,2,1,0:T(8,128)} copy(f32[1,1,1024,128]{3,2,1,0:T(8,128)} %bitcast.11) | data formatting | bytes 1048576
where the time goes:
time: 47.6 us; the launch traced here: 47.4 us
  Pallas kernels  45.6 us (96%)
  local copies, waits for them, and re-layouts  1.87 us (4%)
    pallas_call x1, Pallas kernels, on_device(): pl.pallas_call(functools.partial(kernel, cut_bits, sub_bits, levels, star...  45.6 us
    unnamed x1, local copies, waits for them, and re-layouts  1.87 us

commit v1 on v0

v1 whole, which is shorter than its diff:
```python
import functools

import jax
import jax.numpy as jnp
from jax import lax
from jax.experimental import pallas as pl
from jax.experimental.pallas import tpu as pltpu
from jax.sharding import PartitionSpec as P

MESH = pl.DeviceIdType.MESH
CUTLV = 3
LANES = 128
SEND_ORDER = (4, 0, 1, 2, 3)
STEPS = (
    ("hot", 4), ("hot", 0), ("hot", 1), ("hot", 2), ("hot", 3),
    ("level", 4), ("level", 3), ("level", 0), ("level", 1), ("level", 2),
    "inner", ("end", 4), ("end", 3), ("end", 0), ("end", 1), ("end", 2),
)
BF = jnp.bfloat16
F32 = jnp.float32
I16 = jnp.int16


def dot(a, b):
    return jnp.dot(a, b, preferred_element_type=F32)


def hi_lo(x):
    hi = x.astype(BF)
    lo = (x - hi.astype(F32)).astype(BF)
    return jnp.concatenate([hi, lo], axis=1)


def columns(row):
    n = row.shape[1]
    return jnp.transpose(jnp.broadcast_to(row, (LANES, n)))


def lane_hot(col, half):
    low = (col & (half - 1)).astype(I16)
    lane = lax.broadcasted_iota(jnp.int32, col.shape, 1).astype(I16)
    one, zero = jnp.ones(col.shape, BF), jnp.zeros(col.shape, BF)
    return jnp.concatenate(
        [jnp.where(low == lane + I16(LANES * t), one, zero) for t in range(half // LANES)], axis=1
    )


def choose(col, found, half):
    return jnp.where(col >= half, found[:, LANES:], found[:, :LANES]).astype(BF)


def fold(z):
    return z[:, :LANES] + z[:, LANES:]


def kernel(
    cut_bits, sub_bits, levels, stars, inner,
    res_h, imat_h, iidx_h, dofs_h, fmat_h, fidx_h, cnt_h, out_ref,
    res, imat, iidx, dofs, fmat, fidx, cnt,
    own, far, kept, sent, sent_scale, got, got_scale, acc,
    irow, frow, ihot, fhot, dhot, ghot, gcol, gain, part, ystar,
    lsem, ssem, rsem,
):
    c = lax.axis_index("cut")
    b = lax.axis_index("sub")
    star = fidx.shape[2]
    used = frow.shape[2]
    pad = used // stars
    slab = own.shape[1]
    ndof = res.shape[0]

    def far_device(level):
        if level < CUTLV:
            return (c ^ (1 << (cut_bits - 1 - level)), b)
        return (c, b ^ (1 << (sub_bits - 1 - (level - CUTLV))))

    def upper(level):
        if level < CUTLV:
            return (c >> (cut_bits - 1 - level)) & 1
        return (b >> (sub_bits - 1 - (level - CUTLV))) & 1

    def remote(src, dst, at, level):
        return pltpu.make_async_remote_copy(
            src_ref=src.at[level], dst_ref=dst.at[level],
            send_sem=ssem.at[at + level], recv_sem=rsem.at[at + level],
            device_id=far_device(level), device_id_type=MESH,
        )

    slab_copy = [remote(own, far, 0, level) for level in range(levels)]
    data_copy = [remote(sent, got, levels, level) for level in range(levels)]
    scale_copy = [remote(sent_scale, got_scale, 2 * levels, level) for level in range(levels)]

    barrier = pltpu.get_barrier_semaphore()
    for level in range(levels):
        pl.semaphore_signal(barrier, inc=1, device_id=far_device(level), device_id_type=MESH)
    small = [
        pltpu.make_async_copy(a, d, lsem.at[i])
        for i, (a, d) in enumerate(
            ((dofs_h, dofs), (res_h, res), (fidx_h, fidx), (iidx_h, iidx), (cnt_h, cnt), (imat_h, imat))
        )
    ]
    big = [
        pltpu.make_async_copy(
            fmat_h.at[pl.ds(k * stars, stars)], fmat.at[pl.ds(k * stars, stars)], lsem.at[6 + k]
        )
        for k in range(levels)
    ]
    for copy in small + big:
        copy.start()
    with jax.named_scope("w_in"):
        ystar[...] = jnp.zeros_like(ystar)
        irow[...] = jnp.full_like(irow, -1)
        frow[...] = jnp.full_like(frow, -1)
        small[0].wait()
        small[1].wait()
    wide_res = jnp.concatenate([res[: ndof // 2], res[ndof // 2 :]], axis=1)

    def pick(row):
        found = []
        for r in range(0, row.shape[1], LANES):
            col = columns(row[:, r : r + LANES])
            found.append(choose(col, dot(lane_hot(col, ndof // 2), wide_res), ndof // 2))
        return jnp.concatenate(found, axis=0)

    def slab_step(k, _):
        own[k] = pick(dofs[k])
        return 0

    with jax.named_scope("slabs"):
        lax.fori_loop(0, levels, slab_step, 0)

    with jax.named_scope("barrier"):
        pl.semaphore_wait(barrier, levels)
    for level in SEND_ORDER:
        slab_copy[level].start()

    with jax.named_scope("rows"):
        for i in range(2, 5):
            small[i].wait()
        for n in range(inner):
            irow[:, n * pad : n * pad + star] = iidx[n : n + 1, :]
        for level in range(levels):
            flip = slab * (1 - upper(level))
            live = jnp.broadcast_to(cnt[0:1, level : level + 1], (1, star))
            for j in range(stars):
                row = fidx[level * stars + j] ^ flip
                frow[level, :, j * pad : j * pad + star] = jnp.where(live > j, row, -1)

    block = 2 * LANES

    def row_hot(row, at):
        n = row.shape[1]
        index = jnp.broadcast_to(row - at, (block, n)).astype(I16)
        place = lax.broadcasted_iota(jnp.int32, (block, n), 0).astype(I16)
        return jnp.where(index == place, jnp.ones((block, n), BF), jnp.zeros((block, n), BF))

    def inner_hot(i, _):
        at = pl.multiple_of(i * block, block)
        ihot[pl.ds(at, block), :] = row_hot(irow[...], at)
        return 0

    def make_hots(level):
        def scatter_hot(i, _):
            at = pl.multiple_of(i * block, block)
            fhot[level, pl.ds(at, block), :] = row_hot(frow[level], at)
            dhot[level, pl.ds(at, block), :] = row_hot(dofs[level], at)
            return 0

        with jax.named_scope(f"ghot{level}"):
            for r in range(0, used, LANES):
                col = columns(frow[level, :, r : r + LANES])
                gcol[level, r : r + LANES, :] = col
                ghot[level, r : r + LANES, :] = lane_hot(col, slab)
        with jax.named_scope(f"thot{level}"):
            lax.fori_loop(0, ndof // block, scatter_hot, 0)

    def do_inner():
        with jax.named_scope("ihot"):
            lax.fori_loop(0, ndof // block, inner_hot, 0)
        with jax.named_scope("inner"):
            small[5].wait()
            for n in range(inner):
                g = pick(irow[:, n * pad : (n + 1) * pad])
                y = dot(imat[:, n, :], g[:star])
                ystar[n * pad : n * pad + star, :] = hi_lo(y)
        with jax.named_scope("iscat"):
            for r in range(0, ndof, LANES):
                acc[r : r + LANES, :] = fold(dot(ihot[r : r + LANES, :], ystar[...]))

    def do_level(level):
        with jax.named_scope(f"wslab{level}"):
            big[level].wait()
            slab_copy[level].wait_recv()
        with jax.named_scope(f"solve{level}"):
            wide = jnp.concatenate([far[level], own[level]], axis=1)
            for r in range(0, used, LANES):
                found = dot(ghot[level, r : r + LANES, :], wide)
                gain[r : r + LANES, :] = choose(gcol[level, r : r + LANES, :], found, slab)
            for j in range(stars):
                y = dot(fmat[level * stars + j], gain[j * pad : j * pad + star, :])
                ystar[j * pad : j * pad + star, :] = hi_lo(y)
        with jax.named_scope(f"give{level}"):
            top = jnp.zeros((8, LANES), F32)
            for r in range(0, slab, LANES):
                piece = fold(dot(fhot[level, r : r + LANES, :], ystar[0:used, :]))
                part[r : r + LANES, :] = piece
                top = jnp.maximum(top, jnp.max(jnp.abs(piece.reshape(LANES // 8, 8, LANES)), axis=0))
            sent_scale[level] = top
            scale_copy[level].start()
            scale = jnp.where(top > 0.0, 1.0 / top, 0.0)
            tiles = part[...].reshape(slab // 8, 8, LANES)
            coded = jnp.round((tiles * scale[None]) * 32767.0).astype(jnp.int32)
            sent[level] = coded.reshape(slab, LANES).astype(I16)
            data_copy[level].start()
        with jax.named_scope(f"keep{level}"):
            for r in range(0, slab, LANES):
                kept[level, r : r + LANES, :] = fold(
                    dot(fhot[level, slab + r : slab + r + LANES, :], ystar[0:used, :])
                )

    def finish(level):
        with jax.named_scope(f"wres{level}"):
            scale_copy[level].wait_recv()
            data_copy[level].wait_recv()
        with jax.named_scope(f"fin{level}"):
            tiles = got[level].astype(jnp.int32).astype(F32).reshape(slab // 8, 8, LANES)
            back = (tiles * (1.0 / 32767.0)) * got_scale[level][None]
            both = hi_lo(kept[level] + back.reshape(slab, LANES))
            to = out_ref if level == STEPS[-1][1] else acc
            for r in range(0, ndof, LANES):
                to[r : r + LANES, :] = acc[r : r + LANES, :] + fold(dot(dhot[level, r : r + LANES, :], both))

    for step in STEPS:
        if step == "inner":
            do_inner()
        elif step[0] == "hot":
            make_hots(step[1])
        elif step[0] == "level":
            do_level(step[1])
        else:
            finish(step[1])
    for copy in slab_copy + data_copy + scale_copy:
        copy.wait_send()


def on_device(residual, inner_inverse, inner_index, slab_dofs, face_inverse, face_index, face_count):
    ndof, width = residual.shape[2:]
    inner, star = inner_index.shape[2:]
    levels, slab = slab_dofs.shape[2:]
    stars = face_index.shape[3]
    pad = -(-star // LANES) * LANES
    cut_bits = lax.axis_size("cut").bit_length() - 1
    sub_bits = lax.axis_size("sub").bit_length() - 1
    i32 = jnp.int32
    vm = pltpu.VMEM
    out = pl.pallas_call(
        functools.partial(kernel, cut_bits, sub_bits, levels, stars, inner),
        out_shape=jax.ShapeDtypeStruct((ndof, width), F32),
        in_specs=[pl.BlockSpec(memory_space=pl.ANY)] * 7,
        out_specs=pl.BlockSpec(memory_space=pltpu.VMEM),
        scratch_shapes=[
            vm((ndof, width), BF),
            vm((star, inner, star), BF),
            vm((inner, star), i32),
            vm((levels, 1, slab), i32),
            vm((levels * stars, star, star), BF),
            vm((levels * stars, 1, star), i32),
            vm((1, levels), i32),
            vm((levels, slab, width), BF),
            vm((levels, slab, width), BF),
            vm((levels, slab, width), F32),
            vm((levels, slab, width), jnp.int16),
            vm((levels, 8, width), F32),
            vm((levels, slab, width), jnp.int16),
            vm((levels, 8, width), F32),
            vm((ndof, width), F32),
            vm((1, inner * pad), i32),
            vm((levels, 1, stars * pad), i32),
            vm((ndof, inner * pad), BF),
            vm((levels, ndof, stars * pad), BF),
            vm((levels, ndof, slab), BF),
            vm((levels, stars * pad, slab), BF),
            vm((levels, stars * pad, LANES), i32),
            vm((stars * pad, width), BF),
            vm((slab, width), F32),
            vm((inner * pad, 2 * width), BF),
            pltpu.SemaphoreType.DMA((6 + levels,)),
            pltpu.SemaphoreType.DMA((3 * levels,)),
            pltpu.SemaphoreType.DMA((3 * levels,)),
        ],
        compiler_params=pltpu.CompilerParams(
            collective_id=0, has_side_effects=True, vmem_limit_bytes=60 * 1024 * 1024
        ),
    )(
        residual[0, 0],
        jnp.transpose(inner_inverse[0, 0], (1, 0, 2)),
        inner_index[0, 0],
        slab_dofs[0, 0][:, None, :],
        face_inverse[0, 0].reshape(levels * stars, star, star),
        face_index[0, 0].reshape(levels * stars, 1, star),
        face_count[0],
    )
    return out[None, None]


def solution(mesh):
    return jax.shard_map(
        on_device,
        mesh=mesh,
        in_specs=(
            P("cut", "sub", None, None),
            P("cut", "sub", None, None, None),
            P("cut", "sub", None, None),
            P("cut", "sub", None, None),
            P("cut", "sub", None, None, None, None),
            P("cut", "sub", None, None, None),
            P("cut", "sub", None),
        ),
        out_specs=P("cut", "sub", None, None),
        check_vma=False,
    )
```

time: 47.6 us -> 37.1 us (0.78)
  Pallas kernels: 45.6 us -> 35.1 us
    pallas_call x1, Pallas kernels: 45.6 us -> 35.1 us  [on_device(): pl.pallas_call(functools.partial(kernel, cut_bits, sub_bits, levels, star...]
where the time goes in v1:
time: 37.1 us; the launch traced here: 36.9 us
  Pallas kernels  35.1 us (95%)
  local copies, waits for them, and re-layouts  1.87 us (5%)
    pallas_call x1, Pallas kernels, on_device(): pl.pallas_call(functools.partial(kernel, cut_bits, sub_bits, levels, star...  35.1 us
    unnamed x1, local copies, waits for them, and re-layouts  1.87 us

profile of v1, /device:TPU:1, one launch (start us, length us, event | category | flops | bytes accessed | tf_op | source)
XLA Modules:
  0.0 36.9 jit_solution(16991605864874060278)
XLA Ops:
  0.0 35.1 %shard_map.73 = f32[1024,128]{1,0:T(8,128)} custom-call(bf16[1024,128]{1,0:T(8,128)(2,1)} %bitcast.13, bf16[343,4,343]{2,1,0:T(4,128)(2,1)} %bitcast.12, s32[4,343]{1,0:T(4,128)} %bitcast.16, s32[5,1,512]{2,1,0:T(1,128)} %bitcast.15, bf16[15,343,343]{2,1,0:T(8,128)(2,1)} %bitcast.10, s32[15,1,343]{2,1,0:T(1,128)} %bitcast.14, s32[1,5]{1,0:T(1,128)} %bitcast.17), custom_call_target="tpu_custom_call" | custom-call | tf_op jit(solution)/shard_map/pallas_call | solution.py:256
  35.1 1.9 %copy.9 = f32[1,1,1024,128]{3,2,1,0:T(8,128)} copy(f32[1,1,1024,128]{3,2,1,0:T(8,128)} %bitcast.11) | data formatting | bytes 1048576

commit v2 on v1

--- a/solution.py
+++ b/solution.py
@@ -10,12 +10,10 @@
 MESH = pl.DeviceIdType.MESH
 CUTLV = 3
 LANES = 128
-SEND_ORDER = (4, 0, 1, 2, 3)
-STEPS = (
-    ("hot", 4), ("hot", 0), ("hot", 1), ("hot", 2), ("hot", 3),
-    ("level", 4), ("level", 3), ("level", 0), ("level", 1), ("level", 2),
-    "inner", ("end", 4), ("end", 3), ("end", 0), ("end", 1), ("end", 2),
-)
+SEND = ((4, 0, 1, 2, 3), (4, 1, 2, 0, 3))
+WORK = ((4, 3, 1, 2, 0), (4, 0, 3, 1, 2))
+END = ((4, 3, 0, 1, 2), (4, 3, 1, 2, 0))
+EARLY_HOTS = (4, 0)
 BF = jnp.bfloat16
 F32 = jnp.float32
 I16 = jnp.int16
@@ -69,10 +67,18 @@
     slab = own.shape[1]
     ndof = res.shape[0]
 
-    def far_device(level):
-        if level < CUTLV:
-            return (c ^ (1 << (cut_bits - 1 - level)), b)
-        return (c, b ^ (1 << (sub_bits - 1 - (level - CUTLV))))
+    late = (c >> (cut_bits - 1)) & 1 == 1
+
+    def pick_of(table, i):
+        level = jnp.int32(0)
+        for k, (first, second) in enumerate(zip(*table)):
+            level = jnp.where(i == k, jnp.where(late, second, first), level)
+        return level
+
+    def bit_of(level):
+        on_cut = 1 << jnp.maximum(cut_bits - 1 - level, 0)
+        on_sub = 1 << jnp.minimum(jnp.maximum(sub_bits - 1 - (level - CUTLV), 0), sub_bits)
+        return jnp.where(level < CUTLV, on_cut, 0), jnp.where(level < CUTLV, 0, on_sub)
 
     def upper(level):
         if level < CUTLV:
@@ -80,33 +86,41 @@
         return (b >> (sub_bits - 1 - (level - CUTLV))) & 1
 
     def remote(src, dst, at, level):
+        on_cut, on_sub = bit_of(level)
         return pltpu.make_async_remote_copy(
             src_ref=src.at[level], dst_ref=dst.at[level],
             send_sem=ssem.at[at + level], recv_sem=rsem.at[at + level],
-            device_id=far_device(level), device_id_type=MESH,
+            device_id=(c ^ on_cut, b ^ on_sub), device_id_type=MESH,
         )
 
-    slab_copy = [remote(own, far, 0, level) for level in range(levels)]
-    data_copy = [remote(sent, got, levels, level) for level in range(levels)]
-    scale_copy = [remote(sent_scale, got_scale, 2 * levels, level) for level in range(levels)]
+    def slab_copy(level):
+        return remote(own, far, 0, level)
+
+    def data_copy(level):
+        return remote(sent, got, levels, level)
+
+    def scale_copy(level):
+        return remote(sent_scale, got_scale, 2 * levels, level)
+
+    def matrix_copy(level):
+        return pltpu.make_async_copy(
+            fmat_h.at[pl.ds(level * stars, stars)], fmat.at[pl.ds(level * stars, stars)], lsem.at[6 + level]
+        )
 
     barrier = pltpu.get_barrier_semaphore()
     for level in range(levels):
-        pl.semaphore_signal(barrier, inc=1, device_id=far_device(level), device_id_type=MESH)
+        on_cut, on_sub = bit_of(level)
+        pl.semaphore_signal(barrier, inc=1, device_id=(c ^ on_cut, b ^ on_sub), device_id_type=MESH)
     small = [
         pltpu.make_async_copy(a, d, lsem.at[i])
         for i, (a, d) in enumerate(
             ((dofs_h, dofs), (res_h, res), (fidx_h, fidx), (iidx_h, iidx), (cnt_h, cnt), (imat_h, imat))
         )
     ]
-    big = [
-        pltpu.make_async_copy(
-            fmat_h.at[pl.ds(k * stars, stars)], fmat.at[pl.ds(k * stars, stars)], lsem.at[6 + k]
-        )
-        for k in range(levels)
-    ]
-    for copy in small + big:
+    for copy in small:
         copy.start()
+    for level in range(levels):
+        matrix_copy(level).start()
     with jax.named_scope("w_in"):
         ystar[...] = jnp.zeros_like(ystar)
         irow[...] = jnp.full_like(irow, -1)
@@ -128,11 +142,6 @@
 
     with jax.named_scope("slabs"):
         lax.fori_loop(0, levels, slab_step, 0)
-
-    with jax.named_scope("barrier"):
-        pl.semaphore_wait(barrier, levels)
-    for level in SEND_ORDER:
-        slab_copy[level].start()
 
     with jax.named_scope("rows"):
         for i in range(2, 5):
@@ -159,20 +168,23 @@
         ihot[pl.ds(at, block), :] = row_hot(irow[...], at)
         return 0
 
-    def make_hots(level):
+    def make_hots(i, _):
+        level = pick_of(WORK, i)
+
         def scatter_hot(i, _):
             at = pl.multiple_of(i * block, block)
             fhot[level, pl.ds(at, block), :] = row_hot(frow[level], at)
             dhot[level, pl.ds(at, block), :] = row_hot(dofs[level], at)
             return 0
 
-        with jax.named_scope(f"ghot{level}"):
+        with jax.named_scope("ghot"):
             for r in range(0, used, LANES):
                 col = columns(frow[level, :, r : r + LANES])
                 gcol[level, r : r + LANES, :] = col
                 ghot[level, r : r + LANES, :] = lane_hot(col, slab)
-        with jax.named_scope(f"thot{level}"):
+        with jax.named_scope("thot"):
             lax.fori_loop(0, ndof // block, scatter_hot, 0)
+        return 0
 
     def do_inner():
         with jax.named_scope("ihot"):
@@ -187,11 +199,12 @@
             for r in range(0, ndof, LANES):
                 acc[r : r + LANES, :] = fold(dot(ihot[r : r + LANES, :], ystar[...]))
 
-    def do_level(level):
-        with jax.named_scope(f"wslab{level}"):
-            big[level].wait()
-            slab_copy[level].wait_recv()
-        with jax.named_scope(f"solve{level}"):
+    def do_level(i, _):
+        level = pick_of(WORK, i)
+        with jax.named_scope("wslab"):
+            matrix_copy(level).wait()
+            slab_copy(level).wait_recv()
+        with jax.named_scope("solve"):
             wide = jnp.concatenate([far[level], own[level]], axis=1)
             for r in range(0, used, LANES):
                 found = dot(ghot[level, r : r + LANES, :], wide)
@@ -199,48 +212,57 @@
             for j in range(stars):
                 y = dot(fmat[level * stars + j], gain[j * pad : j * pad + star, :])
                 ystar[j * pad : j * pad + star, :] = hi_lo(y)
-        with jax.named_scope(f"give{level}"):
+        with jax.named_scope("give"):
             top = jnp.zeros((8, LANES), F32)
             for r in range(0, slab, LANES):
                 piece = fold(dot(fhot[level, r : r + LANES, :], ystar[0:used, :]))
                 part[r : r + LANES, :] = piece
                 top = jnp.maximum(top, jnp.max(jnp.abs(piece.reshape(LANES // 8, 8, LANES)), axis=0))
             sent_scale[level] = top
-            scale_copy[level].start()
+            scale_copy(level).start()
             scale = jnp.where(top > 0.0, 1.0 / top, 0.0)
             tiles = part[...].reshape(slab // 8, 8, LANES)
             coded = jnp.round((tiles * scale[None]) * 32767.0).astype(jnp.int32)
             sent[level] = coded.reshape(slab, LANES).astype(I16)
-            data_copy[level].start()
-        with jax.named_scope(f"keep{level}"):
+            data_copy(level).start()
+        with jax.named_scope("keep"):
             for r in range(0, slab, LANES):
                 kept[level, r : r + LANES, :] = fold(
                     dot(fhot[level, slab + r : slab + r + LANES, :], ystar[0:used, :])
                 )
-
-    def finish(level):
-        with jax.named_scope(f"wres{level}"):
-            scale_copy[level].wait_recv()
-            data_copy[level].wait_recv()
-        with jax.named_scope(f"fin{level}"):
+        return 0
+
+    def finish(i, to):
+        level = pick_of(END, i)
+        with jax.named_scope("wres"):
+            scale_copy(level).wait_recv()
+            data_copy(level).wait_recv()
+        with jax.named_scope("fin"):
             tiles = got[level].astype(jnp.int32).astype(F32).reshape(slab // 8, 8, LANES)
             back = (tiles * (1.0 / 32767.0)) * got_scale[level][None]
             both = hi_lo(kept[level] + back.reshape(slab, LANES))
-            to = out_ref if level == STEPS[-1][1] else acc
             for r in range(0, ndof, LANES):
                 to[r : r + LANES, :] = acc[r : r + LANES, :] + fold(dot(dhot[level, r : r + LANES, :], both))
 
-    for step in STEPS:
-        if step == "inner":
-            do_inner()
-        elif step[0] == "hot":
-            make_hots(step[1])
-        elif step[0] == "level":
-            do_level(step[1])
-        else:
-            finish(step[1])
-    for copy in slab_copy + data_copy + scale_copy:
-        copy.wait_send()
+    def add_up(i, _):
+        finish(i, acc)
+        return 0
+
+    early = jnp.where(late, EARLY_HOTS[1], EARLY_HOTS[0])
+    lax.fori_loop(0, early, make_hots, 0)
+    with jax.named_scope("barrier"):
+        pl.semaphore_wait(barrier, levels)
+    for i in range(levels):
+        slab_copy(pick_of(SEND, i)).start()
+    lax.fori_loop(early, levels, make_hots, 0)
+    pl.when(jnp.logical_not(late))(do_inner)
+    lax.fori_loop(0, levels, do_level, 0)
+    pl.when(late)(do_inner)
+    lax.fori_loop(0, levels - 1, add_up, 0)
+    finish(levels - 1, out_ref)
+    for level in range(levels):
+        for copy in (slab_copy, data_copy, scale_copy):
+            copy(level).wait_send()
 
 
 def on_device(residual, inner_inverse, inner_index, slab_dofs, face_inverse, face_index, face_count):
@@ -255,7 +277,7 @@
     vm = pltpu.VMEM
     out = pl.pallas_call(
         functools.partial(kernel, cut_bits, sub_bits, levels, stars, inner),
-        out_shape=jax.ShapeDtypeStruct((ndof, width), F32),
+        out_shape=pltpu.VMEM((ndof, width), F32),
         in_specs=[pl.BlockSpec(memory_space=pl.ANY)] * 7,
         out_specs=pl.BlockSpec(memory_space=pltpu.VMEM),
         scratch_shapes=[

time: 37.1 us -> 34 us (0.916)
  the two profiles are of different devices: /device:TPU:1 before, /device:TPU:240 now
where the time goes in v2:
time: 34 us; the launch traced here: 33.9 us
  Pallas kernels  33.1 us (97%)
  local copies, waits for them, and re-layouts  0.8 us (2%)
    pallas_call x1, Pallas kernels, on_device(): pl.pallas_call(functools.partial(kernel, cut_bits, sub_bits, levels, star...  33.1 us
    unnamed x1, local copies, waits for them, and re-layouts  0.8 us

profile of v2, /device:TPU:240, one launch (start us, length us, event | category | flops | bytes accessed | tf_op | source)
XLA Modules:
  0.0 33.9 jit_solution(18418714008822066128)
XLA Ops:
  0.0 33.1 %shard_map.73 = f32[1024,128]{1,0:T(8,128)S(1)} custom-call(bf16[1024,128]{1,0:T(8,128)(2,1)} %bitcast.13, bf16[343,4,343]{2,1,0:T(4,128)(2,1)} %bitcast.12, s32[4,343]{1,0:T(4,128)} %bitcast.16, s32[5,1,512]{2,1,0:T(1,128)} %bitcast.15, bf16[15,343,343]{2,1,0:T(8,128)(2,1)} %bitcast.11, s32[15,1,343]{2,1,0:T(1,128)} %bitcast.14, s32[1,5]{1,0:T(1,128)} %bitcast.17), custom_call_target="tpu_custom_call" | custom-call | tf_op jit(solution)/shard_map/pallas_call | solution.py:278
  33.1 0.8 %copy.9 = f32[1,1,1024,128]{3,2,1,0:T(8,128)} copy(f32[1,1,1024,128]{3,2,1,0:T(8,128)S(1)} %bitcast.10) | data formatting | bytes 1048576

commit v3 on v2

--- a/solution.py
+++ b/solution.py
@@ -10,10 +10,18 @@
 MESH = pl.DeviceIdType.MESH
 CUTLV = 3
 LANES = 128
-SEND = ((4, 0, 1, 2, 3), (4, 1, 2, 0, 3))
-WORK = ((4, 3, 1, 2, 0), (4, 0, 3, 1, 2))
-END = ((4, 3, 0, 1, 2), (4, 3, 1, 2, 0))
-EARLY_HOTS = (4, 0)
+SEND = ((1, 4, 3, 2), (4, 1, 2, 3))
+BEFORE = (3, 0)
+EARLY_HOTS = (5, 0)
+INNER_AT = ((0, 1), (0, 1))
+WORK = (
+    (4, 3, 1, 2, 0), (4, 3, 1, 2, 0), (4, 3, 1, 2, 0), (4, 3, 1, 0, 2),
+    (4, 0, 3, 1, 2), (4, 0, 3, 1, 2), (4, 0, 3, 1, 2), (4, 0, 3, 1, 2),
+)
+END = (
+    (4, 3, 0, 2, 1), (4, 3, 1, 0, 2), (4, 3, 1, 0, 2), (4, 3, 1, 0, 2),
+    (4, 3, 2, 0, 1), (4, 3, 1, 2, 0), (4, 3, 1, 2, 0), (4, 3, 1, 2, 0),
+)
 BF = jnp.bfloat16
 F32 = jnp.float32
 I16 = jnp.int16
@@ -56,8 +64,8 @@
     res_h, imat_h, iidx_h, dofs_h, fmat_h, fidx_h, cnt_h, out_ref,
     res, imat, iidx, dofs, fmat, fidx, cnt,
     own, far, kept, sent, sent_scale, got, got_scale, acc,
-    irow, frow, ihot, fhot, dhot, ghot, gcol, gain, part, ystar,
-    lsem, ssem, rsem,
+    irow, frow, ihot, fhot, dhot, ghot, gcol, gain, part, ystar, istar,
+    lsem, ssem, rsem, near_ok, far_ok,
 ):
     c = lax.axis_index("cut")
     b = lax.axis_index("sub")
@@ -69,11 +77,18 @@
 
     late = (c >> (cut_bits - 1)) & 1 == 1
 
-    def pick_of(table, i):
-        level = jnp.int32(0)
-        for k, (first, second) in enumerate(zip(*table)):
-            level = jnp.where(i == k, jnp.where(late, second, first), level)
-        return level
+    place = c >> (cut_bits - 3)
+
+    def order_of(table):
+        code = jnp.int32(0)
+        for k, order in enumerate(table):
+            code = jnp.where(place == k, sum(level << 3 * i for i, level in enumerate(order)), code)
+        return code
+
+    work_order, end_order = order_of(WORK), order_of(END)
+
+    def nth(order, i):
+        return (order >> 3 * i) & 7
 
     def bit_of(level):
         on_cut = 1 << jnp.maximum(cut_bits - 1 - level, 0)
@@ -108,9 +123,19 @@
         )
 
     barrier = pltpu.get_barrier_semaphore()
-    for level in range(levels):
+    first = b & 1 == 0
+    other = (c, b ^ 1)
+    for level in range(1, levels):
         on_cut, on_sub = bit_of(level)
-        pl.semaphore_signal(barrier, inc=1, device_id=(c ^ on_cut, b ^ on_sub), device_id_type=MESH)
+        pl.semaphore_signal(
+            barrier, inc=1, device_id=(c ^ on_cut, (b ^ on_sub) & ~1), device_id_type=MESH
+        )
+
+    @pl.when(jnp.logical_not(first))
+    def _():
+        pl.semaphore_signal(barrier, inc=1, device_id=other, device_id_type=MESH)
+
+    pl.semaphore_signal(barrier, inc=1, device_id=(c ^ bit_of(0)[0], b | 1), device_id_type=MESH)
     small = [
         pltpu.make_async_copy(a, d, lsem.at[i])
         for i, (a, d) in enumerate(
@@ -123,6 +148,7 @@
         matrix_copy(level).start()
     with jax.named_scope("w_in"):
         ystar[...] = jnp.zeros_like(ystar)
+        istar[...] = jnp.zeros_like(istar)
         irow[...] = jnp.full_like(irow, -1)
         frow[...] = jnp.full_like(frow, -1)
         small[0].wait()
@@ -169,7 +195,7 @@
         return 0
 
     def make_hots(i, _):
-        level = pick_of(WORK, i)
+        level = nth(work_order, i)
 
         def scatter_hot(i, _):
             at = pl.multiple_of(i * block, block)
@@ -186,21 +212,26 @@
             lax.fori_loop(0, ndof // block, scatter_hot, 0)
         return 0
 
-    def do_inner():
-        with jax.named_scope("ihot"):
+    def inner_stars(begin, end):
+        for n in range(begin, end):
+            g = pick(irow[:, n * pad : (n + 1) * pad])
+            y = dot(imat[:, n, :], g[:star])
+            istar[n * pad : n * pad + star, :] = hi_lo(y)
+
+    def inner_begin():
+        with jax.named_scope("innera"):
+            small[5].wait()
             lax.fori_loop(0, ndof // block, inner_hot, 0)
-        with jax.named_scope("inner"):
-            small[5].wait()
-            for n in range(inner):
-                g = pick(irow[:, n * pad : (n + 1) * pad])
-                y = dot(imat[:, n, :], g[:star])
-                ystar[n * pad : n * pad + star, :] = hi_lo(y)
-        with jax.named_scope("iscat"):
+            inner_stars(0, inner // 2)
+
+    def inner_end():
+        with jax.named_scope("innerb"):
+            inner_stars(inner // 2, inner)
             for r in range(0, ndof, LANES):
-                acc[r : r + LANES, :] = fold(dot(ihot[r : r + LANES, :], ystar[...]))
+                acc[r : r + LANES, :] = fold(dot(ihot[r : r + LANES, :], istar[...]))
 
     def do_level(i, _):
-        level = pick_of(WORK, i)
+        level = nth(work_order, i)
         with jax.named_scope("wslab"):
             matrix_copy(level).wait()
             slab_copy(level).wait_recv()
@@ -233,7 +264,7 @@
         return 0
 
     def finish(i, to):
-        level = pick_of(END, i)
+        level = nth(end_order, i)
         with jax.named_scope("wres"):
             scale_copy(level).wait_recv()
             data_copy(level).wait_recv()
@@ -248,16 +279,60 @@
         finish(i, acc)
         return 0
 
+    with jax.named_scope("near"):
+
+        @pl.when(first)
+        def _():
+            pl.semaphore_wait(barrier, 2 * (levels - 1) + 1)
+            pl.semaphore_signal(near_ok, inc=1, device_id=other, device_id_type=MESH)
+
+        @pl.when(jnp.logical_not(first))
+        def _():
+            pl.semaphore_wait(near_ok, 1)
+
+    def meet_far():
+        with jax.named_scope("barrier"):
+
+            @pl.when(jnp.logical_not(first))
+            def _():
+                pl.semaphore_wait(barrier, 2)
+                pl.semaphore_signal(far_ok, inc=1, device_id=other, device_id_type=MESH)
+
+            @pl.when(first)
+            def _():
+                pl.semaphore_wait(far_ok, 1)
+
+        slab_copy(0).start()
+
+    def send_near(begin, end, half):
+        for i in range(begin, end):
+            slab_copy(SEND[half][i]).start()
+
+    @pl.when(late)
+    def _():
+        send_near(0, BEFORE[1], 1)
+        meet_far()
+        send_near(BEFORE[1], levels - 1, 1)
+
+    @pl.when(jnp.logical_not(late))
+    def _():
+        send_near(0, BEFORE[0], 0)
+
     early = jnp.where(late, EARLY_HOTS[1], EARLY_HOTS[0])
     lax.fori_loop(0, early, make_hots, 0)
-    with jax.named_scope("barrier"):
-        pl.semaphore_wait(barrier, levels)
-    for i in range(levels):
-        slab_copy(pick_of(SEND, i)).start()
+
+    @pl.when(jnp.logical_not(late))
+    def _():
+        meet_far()
+        send_near(BEFORE[0], levels - 1, 0)
+
     lax.fori_loop(early, levels, make_hots, 0)
-    pl.when(jnp.logical_not(late))(do_inner)
-    lax.fori_loop(0, levels, do_level, 0)
-    pl.when(late)(do_inner)
+    split = [jnp.where(late, INNER_AT[1][k], INNER_AT[0][k]) for k in range(2)]
+    lax.fori_loop(0, split[0], do_level, 0)
+    inner_begin()
+    lax.fori_loop(split[0], split[1], do_level, 0)
+    inner_end()
+    lax.fori_loop(split[1], levels, do_level, 0)
     lax.fori_loop(0, levels - 1, add_up, 0)
     finish(levels - 1, out_ref)
     for level in range(levels):
@@ -305,10 +380,13 @@
             vm((levels, stars * pad, LANES), i32),
             vm((stars * pad, width), BF),
             vm((slab, width), F32),
+            vm((stars * pad, 2 * width), BF),
             vm((inner * pad, 2 * width), BF),
             pltpu.SemaphoreType.DMA((6 + levels,)),
             pltpu.SemaphoreType.DMA((3 * levels,)),
             pltpu.SemaphoreType.DMA((3 * levels,)),
+            pltpu.SemaphoreType.REGULAR,
+            pltpu.SemaphoreType.REGULAR,
         ],
         compiler_params=pltpu.CompilerParams(
             collective_id=0, has_side_effects=True, vmem_limit_bytes=60 * 1024 * 1024

time: 34 us -> 33.6 us (0.988)
  the two profiles are of different devices: /device:TPU:240 before, /device:TPU:1 now
where the time goes in v3:
time: 33.6 us; the launch traced here: 33.5 us
  Pallas kernels  32.7 us (97%)
  local copies, waits for them, and re-layouts  0.8 us (2%)
    pallas_call x1, Pallas kernels, on_device(): pl.pallas_call(functools.partial(kernel, cut_bits, sub_bits, levels, star...  32.7 us
    unnamed x1, local copies, waits for them, and re-layouts  0.8 us

profile of v3, /device:TPU:1, one launch (start us, length us, event | category | flops | bytes accessed | tf_op | source)
XLA Modules:
  0.0 33.5 jit_solution(9995857220103906455)
XLA Ops:
  0.0 32.7 %shard_map.73 = f32[1024,128]{1,0:T(8,128)S(1)} custom-call(bf16[1024,128]{1,0:T(8,128)(2,1)} %bitcast.13, bf16[343,4,343]{2,1,0:T(4,128)(2,1)} %bitcast.12, s32[4,343]{1,0:T(4,128)} %bitcast.16, s32[5,1,512]{2,1,0:T(1,128)} %bitcast.15, bf16[15,343,343]{2,1,0:T(8,128)(2,1)} %bitcast.11, s32[15,1,343]{2,1,0:T(1,128)} %bitcast.14, s32[1,5]{1,0:T(1,128)} %bitcast.17), custom_call_target="tpu_custom_call" | custom-call | tf_op jit(solution)/shard_map/pallas_call | solution.py:353
  32.7 0.8 %copy.9 = f32[1,1,1024,128]{3,2,1,0:T(8,128)} copy(f32[1,1,1024,128]{3,2,1,0:T(8,128)S(1)} %bitcast.10) | data formatting | bytes 1048576

commit v4 on v3

--- a/solution.py
+++ b/solution.py
@@ -15,8 +15,8 @@
 EARLY_HOTS = (5, 0)
 INNER_AT = ((0, 1), (0, 1))
 WORK = (
-    (4, 3, 1, 2, 0), (4, 3, 1, 2, 0), (4, 3, 1, 2, 0), (4, 3, 1, 0, 2),
-    (4, 0, 3, 1, 2), (4, 0, 3, 1, 2), (4, 0, 3, 1, 2), (4, 0, 3, 1, 2),
+    (4, 3, 1, 2, 0), (4, 1, 3, 2, 0), (4, 1, 3, 2, 0), (4, 1, 3, 0, 2),
+    (4, 0, 3, 1, 2), (4, 0, 1, 3, 2), (4, 0, 1, 3, 2), (4, 0, 1, 3, 2),
 )
 END = (
     (4, 3, 0, 2, 1), (4, 3, 1, 0, 2), (4, 3, 1, 0, 2), (4, 3, 1, 0, 2),

time: 33.6 us -> 33.4 us (level)
  Pallas kernels: 32.7 us -> 32.3 us
    pallas_call x1, Pallas kernels: 32.7 us -> 32.3 us  [on_device(): pl.pallas_call(functools.partial(kernel, cut_bits, sub_bits, levels, star...]
where the time goes in v4:
time: 33.4 us; the launch traced here: 33.2 us
  Pallas kernels  32.3 us (97%)
  local copies, waits for them, and re-layouts  0.8 us (2%)
    pallas_call x1, Pallas kernels, on_device(): pl.pallas_call(functools.partial(kernel, cut_bits, sub_bits, levels, star...  32.3 us
    unnamed x1, local copies, waits for them, and re-layouts  0.8 us

profile of v4, /device:TPU:1, one launch (start us, length us, event | category | flops | bytes accessed | tf_op | source)
XLA Modules:
  0.0 33.2 jit_solution(4560535871526557555)
XLA Ops:
  0.0 32.3 %shard_map.73 = f32[1024,128]{1,0:T(8,128)S(1)} custom-call(bf16[1024,128]{1,0:T(8,128)(2,1)} %bitcast.13, bf16[343,4,343]{2,1,0:T(4,128)(2,1)} %bitcast.12, s32[4,343]{1,0:T(4,128)} %bitcast.16, s32[5,1,512]{2,1,0:T(1,128)} %bitcast.15, bf16[15,343,343]{2,1,0:T(8,128)(2,1)} %bitcast.11, s32[15,1,343]{2,1,0:T(1,128)} %bitcast.14, s32[1,5]{1,0:T(1,128)} %bitcast.17), custom_call_target="tpu_custom_call" | custom-call | tf_op jit(solution)/shard_map/pallas_call | solution.py:353
  32.4 0.8 %copy.9 = f32[1,1,1024,128]{3,2,1,0:T(8,128)} copy(f32[1,1,1024,128]{3,2,1,0:T(8,128)S(1)} %bitcast.10) | data formatting | bytes 1048576
